TPU v7x, 128 devices: a whole 4x4x4 slice. The times are simulated.
128 devices in a mesh: gz: 128 (over y, x, z, core).
Axes of the slice: x: 4, y: 4, z: 4, core: 2. Of those that a mesh axis runs over, the one named last changes fastest.
Arguments:
- u_face: float32 [256, 1024, 512], P('gz')
- v_face: float32 [256, 1024, 512], P('gz')
- w_face: float32 [256, 1024, 512], P('gz')
- smoke: float32 [256, 1024, 512], P('gz'), may hold values from 0 to 2
- obstacles: int32 [256, 32, 512], P('gz'), may hold values from -2147483648 to 2147483647, as said below
Outputs:
- impulse: float32 [256, 1024, 512], P('gz')
- relative_residual: float32 [256, 1024, 512], P('gz')
Inputs may be any that keep to these rules, and one draw needn't show every extreme that they name: Bit k of obstacles[z, b, x] is 1 where cell (z, 32 b + k, x) is solid and 0 where it holds fluid; every bit of a word is used.
All inputs are finite; a program needn't handle non-finite values. Where the computation divides by a largest or mean magnitude, that divisor is 1e-20 or more.
Results may differ from a plain program's by a relative error of at most 0.00011.
Values sent between devices are 32-bit elements; how exact they have to be, the bound alone decides.
A program may use at most 192 MiB of HBM per device.

v0:
```python
import functools

import jax
import jax.numpy as jnp
from jax import lax
from jax.sharding import Mesh
from jax.sharding import PartitionSpec as P

ITERS = 2
GZ = ("gz_0", "gz_1", "gz_2", "gz_3")


EPS = 1e-06
CFL = 0.5
BUOYANCY = 100.0


def with_halo(block, sides, width):
    for axis, dim in sides:
        count = lax.axis_size(axis)
        forward = [(i, i + 1) for i in range(count - 1)]
        backward = [(target, source) for source, target in forward]
        low = lax.ppermute(
            lax.slice_in_dim(block, block.shape[dim] - width, None, axis=dim), axis, forward
        )
        high = lax.ppermute(lax.slice_in_dim(block, 0, width, axis=dim), axis, backward)
        block = jnp.concatenate([low, block, high], axis=dim)
    return block


def by_axis(x, axes):
    return functools.reduce(lax.psum, axes, x)


def shifted(x, axis, by):
    devices = lax.axis_size(axis)
    pairs = [(i, i + by) for i in range(devices) if 0 <= i + by < devices]
    return lax.ppermute(x, axis, pairs)


def over_axes(x, axes):
    for axis in axes:
        x = lax.pmax(x, axis)
    return x


def unpack_flags(packed):
    places = jnp.arange(32, dtype=jnp.int32)
    flags = jnp.right_shift(packed[:, :, None, :], places[None, None, :, None]) & 1
    return flags.reshape(packed.shape[0], packed.shape[1] * 32, packed.shape[2])


def later_cells(field, axis):
    size = field.shape[axis]
    tail = lax.slice_in_dim(field, 1, size, axis=axis)
    shape = list(field.shape)
    shape[axis] = 1
    return jnp.concatenate([tail, jnp.zeros(shape, field.dtype)], axis)


def earlier_cells(field, axis):
    size = field.shape[axis]
    head = lax.slice_in_dim(field, 0, size - 1, axis=axis)
    shape = list(field.shape)
    shape[axis] = 1
    return jnp.concatenate([jnp.zeros(shape, field.dtype), head], axis)


def in_plane(field):
    return (
        later_cells(field, 1)
        + earlier_cells(field, 1)
        + later_cells(field, 2)
        + earlier_cells(field, 2)
    )


def apply_operator(search, fluid_cells, solid_cells, open_count):
    masked = search * fluid_cells
    padded = with_halo(masked, ((GZ, 0),), 1)
    beside_all = padded[2:] + padded[:-2] + in_plane(masked)
    return fluid_cells * (open_count * search - beside_all) + solid_cells * search


def paired_sums(residual, precond, image):
    return (by_axis(jnp.sum(residual * precond), GZ), by_axis(jnp.sum(image * precond), GZ))


def local(u_face, v_face, w_face, smoke, obstacles):
    rimmed = with_halo(obstacles, ((GZ, 0),), 1)
    solid_full = unpack_flags(rimmed).astype(jnp.float32)
    solid_cells = solid_full[1:-1]
    fluid_cells = 1.0 - solid_cells
    lowest = jnp.concatenate([w_face[0:1], smoke[0:1]], 0)
    arrived = shifted(lowest, GZ, -1)
    w_next = jnp.concatenate([w_face[1:], arrived[0:1]], 0)
    smoke_next = jnp.concatenate([smoke[1:], arrived[1:2]], 0)
    around_solid = solid_full[2:] + solid_full[:-2] + in_plane(solid_cells)
    open_count = 6.0 - around_solid
    scaling = fluid_cells * jnp.maximum(open_count, 1.0) + solid_cells
    local_fastest = jnp.maximum(
        jnp.maximum(jnp.max(jnp.abs(u_face)), jnp.max(jnp.abs(v_face))), jnp.max(jnp.abs(w_face))
    )
    flat_part = later_cells(u_face, 2) - u_face + (later_cells(v_face, 1) - v_face)
    count_part = jnp.sum(fluid_cells)
    fastest = over_axes(local_fastest, GZ)
    time_step = CFL / (fastest + EPS)
    lift = time_step * BUOYANCY
    lifted_w = w_face + lift * smoke
    lifted_next = w_next + lift * smoke_next
    divergence = fluid_cells * (flat_part + (lifted_next - lifted_w))
    div_part = jnp.sum(divergence * divergence)
    partials = (div_part, count_part)
    totals = (by_axis(partials[0], GZ), by_axis(partials[1], GZ))
    div_squares = totals[0]
    fluid_total = jnp.maximum(totals[1], 1.0)
    residual = divergence / time_step
    solution = jnp.zeros_like(residual)
    precond = residual / scaling
    image = apply_operator(precond, fluid_cells, solid_cells, open_count)
    gamma_now, delta_now = paired_sums(residual, precond, image)
    alpha = gamma_now / delta_now
    beta_now = jnp.zeros_like(alpha)
    search = precond
    along = image
    for step in range(ITERS):
        if step > 0:
            search = precond + beta_now * search
            along = image + beta_now * along
        solution = solution + alpha * search
        residual = residual - alpha * along
        if step + 1 < ITERS:
            precond = residual / scaling
            image = apply_operator(precond, fluid_cells, solid_cells, open_count)
            gamma_next, delta_now = paired_sums(residual, precond, image)
            beta_now = gamma_next / gamma_now
            alpha = gamma_next / (delta_now - beta_now * gamma_next / alpha)
            gamma_now = gamma_next
    impulse = time_step * solution
    relative_residual = residual * time_step / jnp.sqrt(div_squares / fluid_total + EPS)
    return (impulse, relative_residual)


def solution(mesh):
    torus = Mesh(mesh.devices.reshape(4, 4, 4, 2), ("gz_0", "gz_1", "gz_2", "gz_3"))
    placed = (
        P(GZ, None, None),
        P(GZ, None, None),
        P(GZ, None, None),
        P(GZ, None, None),
        P(GZ, None, None),
    )
    return jax.shard_map(
        local,
        mesh=torus,
        in_specs=placed,
        out_specs=(P(GZ, None, None), P(GZ, None, None)),
        check_vma=False,
    )
```

profile of v0, /device:TPU:1, one launch (start us, length us, event | category | flops | bytes accessed | tf_op | source)
XLA Modules:
  0.0 329.5 jit_solution(10203803512828236046)
XLA Ops:
  0.6 2.8 fusion.36
  4.1 1.8 fusion.34
  5.9 2.6 pad_maximum_fusion.4
  8.5 3.5 %collective-permute-start.2 = (f32[2,1024,512]{2,1,0:T(8,128)}, f32[2,1024,512]{2,1,0:T(8,128)}, u32[]{:S(2)}, u32[]{:S(2)}) collective-permute-start(f32[2,1024,512]{2,1,0:T(8,128)} %pad_maximum_fusion.4), channel_id=1, source_target_pairs={{1,0},{2,1},{3,2},{4,3},{5,4},{6,5},{7,6},{8,7},{9,8},{10,9},{11,1... | collective-permute-start | bytes 12582920 | tf_op jit(solution)/shard_map/ppermute | solution.py:38
  12.0 3.6 %collective-permute-start = (s32[1,32,512]{2,1,0:T(8,128)S(1)}, s32[1,32,512]{2,1,0:T(8,128)S(1)}, u32[]{:S(2)}, u32[]{:S(2)}) collective-permute-start(s32[1,32,512]{2,1,0:T(8,128)S(1)} %get-tuple-element.62), channel_id=1, source_target_pairs={{0,1},{1,2},{2,3},{3,4},{4,5},{5,6},{6,7},{7,8},{8,9},{9,10},{10,1... | collective-permute-start | bytes 196616 | tf_op jit(solution)/shard_map/ppermute | solution.py:23
  15.6 1.9 collective-permute-start.1
  17.5 1.7 abs_reduce_fusion.1
  19.2 1.0 abs_reduce_fusion
  22.1 13.6 %pmax.28 = f32[]{:T(128)} all-reduce(f32[]{:T(128)S(6)} %max.21), channel_id=1, replica_groups=mesh['gz_0'=4,'gz_1'=4,'gz_2'=4,'gz_3'=2] {'gz_0'}, use_global_device_ids=true, to_apply=%region_3.0 | all-reduce | flops 1 | bytes 8 | tf_op jit(solution)/shard_map/pmax | solution.py:43
  35.7 7.0 %pmax.29 = f32[]{:T(128)} all-reduce(f32[]{:T(128)} %pmax.28), channel_id=1, replica_groups=mesh['gz_0'=4,'gz_1'=4,'gz_2'=4,'gz_3'=2] {'gz_1'}, use_global_device_ids=true, to_apply=%region_4.0 | all-reduce | flops 1 | bytes 8 | tf_op jit(solution)/shard_map/pmax | solution.py:43
  42.7 11.1 %pmax.30 = f32[]{:T(128)} all-reduce(f32[]{:T(128)} %pmax.29), channel_id=1, replica_groups=mesh['gz_0'=4,'gz_1'=4,'gz_2'=4,'gz_3'=2] {'gz_2'}, use_global_device_ids=true, to_apply=%region_5.0 | all-reduce | flops 1 | bytes 8 | tf_op jit(solution)/shard_map/pmax | solution.py:43
  53.8 23.9 %pmax.31 = f32[]{:T(128)} all-reduce(f32[]{:T(128)} %pmax.30), channel_id=1, replica_groups=mesh['gz_0'=4,'gz_1'=4,'gz_2'=4,'gz_3'=2] {'gz_3'}, use_global_device_ids=true, to_apply=%region_6.0 | all-reduce | flops 1 | bytes 8 | tf_op jit(solution)/shard_map/pmax | solution.py:43
  77.7 5.4 %slice.110 = f32[2,1024,511]{2,1,0:T(8,128)} slice(f32[2,1024,512]{2,1,0:T(8,128)} %param.5), slice={[0:2], [0:1024], [1:512]} | slice | bytes 8372224 | tf_op jit(solution)/shard_map/slice | solution.py:55
  83.1 2.5 slice.111
  86.4 0.9 fusion.1
  87.3 5.1 %fusion.27 = (f32[2,1024,511]{2,1,0:T(8,128)}, f32[2,1024,511]{2,1,0:T(8,128)}) fusion(f32[4,1024,512]{2,1,0:T(8,128)S(1)} %fusion.1), kind=kLoop, calls=%fused_computation.47 | loop fusion | bytes 16744448 | tf_op jit(solution)/shard_map/slice | solution.py:55
  92.4 0.6 copy-done
  93.0 4.3 %fusion.26 = (f32[2,1023,512]{2,1,0:T(8,128)}, f32[2,1023,512]{2,1,0:T(8,128)}) fusion(f32[4,1024,512]{2,1,0:T(8,128)S(1)} %fusion.1), kind=kLoop, calls=%fused_computation.46 | loop fusion | bytes 16760832 | tf_op jit(solution)/shard_map/slice | solution.py:55
  97.3 4.8 %fusion.35 = (f32[1,1024,512]{2,1,0:T(8,128)}, f32[1,1024,512]{2,1,0:T(8,128)}) fusion(f32[2,1024,512]{2,1,0:T(8,128)} %collective-permute-done.2), kind=kLoop, calls=%fused_computation.55 | loop fusion | bytes 8388608 | tf_op jit(solution)/shard_map/slice | solution.py:96
  102.1 27.6 %fusion.19 = (f32[2,1024,512]{2,1,0:T(8,128)}, f32[2,1024,512]{2,1,0:T(8,128)}, f32[2,1024,512]{2,1,0:T(8,128)}, f32[2,1024,512]{2,1,0:T(8,128)}) fusion(f32[4,1024,512]{2,1,0:T(8,128)} %copy-done, f32[]{:T(128)S(6)} %div.34, f32[2,1024,512]{2,1,0:T(8,128)} %param.7, f32[2,1024,512]{2,1,0:T(8,128)} %param.8, f32[1,1024,512]{2,1,0:T(8,128)} %get-tuple-element.59, ...), kind=kLoop, calls=%fused_computation.43 | loop fusion | flops 26214400 | bytes 79654920 | tf_op jit(solution)/shard_map/mul | solution.py:79
  129.7 2.8 fusion.31
  132.5 2.3 collective-permute-start.3
  134.8 3.8 %collective-permute-start.4 = (f32[1,1024,512]{2,1,0:T(8,128)S(1)}, f32[1,1024,512]{2,1,0:T(8,128)}, u32[]{:S(2)}, u32[]{:S(2)}) collective-permute-start(f32[1,1024,512]{2,1,0:T(8,128)S(1)} %get-tuple-element.51), channel_id=1, source_target_pairs={{0,1},{1,2},{2,3},{3,4},{4,5},{5,6},{6,7},{7,8},{8,9},{9,10},{10,1... | collective-permute-start | bytes 6291464 | tf_op jit(solution)/shard_map/ppermute | solution.py:23
  138.6 4.9 %fusion.33 = (f32[2,1024,511]{2,1,0:T(8,128)}, f32[2,1024,511]{2,1,0:T(8,128)}) fusion(f32[2,1024,512]{2,1,0:T(8,128)S(1)} %copy-done.1), kind=kLoop, calls=%fused_computation.53 | loop fusion | bytes 16744448 | tf_op jit(solution)/shard_map/slice | solution.py:55
  143.4 4.1 %fusion.32 = (f32[2,1023,512]{2,1,0:T(8,128)}, f32[2,1023,512]{2,1,0:T(8,128)}) fusion(f32[2,1024,512]{2,1,0:T(8,128)S(1)} %copy-done.1), kind=kLoop, calls=%fused_computation.52 | loop fusion | bytes 16760832 | tf_op jit(solution)/shard_map/slice | solution.py:55
  147.5 12.6 %collective-permute-done.3 = f32[1,1024,512]{2,1,0:T(8,128)S(1)} collective-permute-done((f32[1,1024,512]{2,1,0:T(8,128)S(1)}, f32[1,1024,512]{2,1,0:T(8,128)S(1)}, u32[]{:S(2)}, u32[]{:S(2)}) %collective-permute-start.3) | collective-permute-done | bytes 2097184 | tf_op jit(solution)/shard_map/ppermute | solution.py:26
  160.1 1.2 collective-permute-done.4
  161.3 16.2 %multiply_reduce_fusion.3 = (f32[]{:T(128)}, f32[]{:T(128)}, f32[2,1024,512]{2,1,0:T(8,128)}, f32[]{:T(128)}) fusion(f32[2,1024,512]{2,1,0:T(8,128)} %get-tuple-element.36, f32[2,1024,512]{2,1,0:T(8,128)} %get-tuple-element.37, f32[]{:T(128)S(6)} %div.34, f32[2,1024,511]{2,1,0:T(8,128)} %get-tuple-element.55, f32[2,1024,511]{2,1,0:T(8,128)} %get-tuple-element.54, ...), kind=kLoop, calls=%fused_computation.32 | loop fusion | flops 19922944 | bytes 46112784 | tf_op jit(solution)/shard_map/reduce_sum | solution.py:86
  177.5 13.8 %all-reduce.19 = (f32[]{:T(128)}, f32[]{:T(128)}) all-reduce(f32[]{:T(128)} %get-tuple-element.6, f32[]{:T(128)} %get-tuple-element.5), channel_id=1, replica_groups=mesh['gz_0'=4,'gz_1'=4,'gz_2'=4,'gz_3'=2] {'gz_0'}, use_global_device_ids=true, to_apply=%region_8.0 | all-reduce | flops 2 | bytes 16 | tf_op jit(solution)/shard_map/psum | solution.py:32
  191.3 6.6 %all-reduce.17 = (f32[]{:T(128)}, f32[]{:T(128)}) all-reduce(f32[]{:T(128)} %get-tuple-element.23, f32[]{:T(128)} %get-tuple-element.24), channel_id=1, replica_groups=mesh['gz_0'=4,'gz_1'=4,'gz_2'=4,'gz_3'=2] {'gz_1'}, use_global_device_ids=true, to_apply=%region_9.0 | all-reduce | flops 2 | bytes 16 | tf_op jit(solution)/shard_map/psum | solution.py:32
  197.9 10.2 %all-reduce.15 = (f32[]{:T(128)}, f32[]{:T(128)}) all-reduce(f32[]{:T(128)} %get-tuple-element.17, f32[]{:T(128)} %get-tuple-element.18), channel_id=1, replica_groups=mesh['gz_0'=4,'gz_1'=4,'gz_2'=4,'gz_3'=2] {'gz_2'}, use_global_device_ids=true, to_apply=%region_10.0 | all-reduce | flops 2 | bytes 16 | tf_op jit(solution)/shard_map/psum | solution.py:32
  208.1 11.0 %all-reduce.21 = (f32[]{:T(128)}, f32[]{:T(128)}) all-reduce(f32[]{:T(128)} %get-tuple-element.11, f32[]{:T(128)} %get-tuple-element.12), channel_id=1, replica_groups=mesh['gz_0'=4,'gz_1'=4,'gz_2'=4,'gz_3'=2] {'gz_3'}, use_global_device_ids=true, to_apply=%region_11.0 | all-reduce | flops 2 | bytes 16 | tf_op jit(solution)/shard_map/psum | solution.py:32
  220.4 8.9 %fusion.18 = (f32[2,1024,512]{2,1,0:T(8,128)S(1)}, f32[2,1024,512]{2,1,0:T(8,128)}) fusion(f32[4,1024,512]{2,1,0:T(8,128)} %copy-done, f32[2,1024,512]{2,1,0:T(8,128)} %get-tuple-element.38, f32[2,1024,512]{2,1,0:T(8,128)} %get-tuple-element.34, f32[]{:T(128)S(6)} %div.37, f32[2,1024,512]{2,1,0:T(8,128)} %get-tuple-element.37, f32[]{:T(128)S(6)} %div.34), kind=kLoop, calls=%fused_computation.42 | loop fusion | flops 9437184 | bytes 25165832 | tf_op jit(solution)/shard_map/mul | solution.py:79
  229.3 2.4 fusion.28
  231.6 2.2 collective-permute-start.5
  233.9 3.5 %collective-permute-start.6 = (f32[1,1024,512]{2,1,0:T(8,128)}, f32[1,1024,512]{2,1,0:T(8,128)}, u32[]{:S(2)}, u32[]{:S(2)}) collective-permute-start(f32[1,1024,512]{2,1,0:T(8,128)} %get-tuple-element.45), channel_id=1, source_target_pairs={{0,1},{1,2},{2,3},{3,4},{4,5},{5,6},{6,7},{7,8},{8,9},{9,10},{10,1... | collective-permute-start | bytes 6291464 | tf_op jit(solution)/shard_map/ppermute | solution.py:23
  237.4 4.8 %fusion.30 = (f32[2,1024,511]{2,1,0:T(8,128)}, f32[2,1024,511]{2,1,0:T(8,128)}) fusion(f32[2,1024,512]{2,1,0:T(8,128)S(1)} %get-tuple-element.32), kind=kLoop, calls=%fused_computation.50 | loop fusion | bytes 16744448 | tf_op jit(solution)/shard_map/slice | solution.py:55
  242.3 4.9 %fusion.29 = (f32[2,1023,512]{2,1,0:T(8,128)}, f32[2,1023,512]{2,1,0:T(8,128)}) fusion(f32[2,1024,512]{2,1,0:T(8,128)S(1)} %get-tuple-element.32), kind=kLoop, calls=%fused_computation.49 | loop fusion | bytes 16760832 | tf_op jit(solution)/shard_map/slice | solution.py:55
  247.2 12.3 %collective-permute-done.5 = f32[1,1024,512]{2,1,0:T(8,128)} collective-permute-done((f32[1,1024,512]{2,1,0:T(8,128)}, f32[1,1024,512]{2,1,0:T(8,128)}, u32[]{:S(2)}, u32[]{:S(2)}) %collective-permute-start.5) | collective-permute-done | bytes 2097184 | tf_op jit(solution)/shard_map/ppermute | solution.py:26
  259.5 1.2 collective-permute-done.6
  260.7 13.8 %multiply_reduce_fusion = (f32[]{:T(128)}, f32[]{:T(128)}, f32[]{:T(128)}, f32[2,1024,512]{2,1,0:T(8,128)}) fusion(f32[2,1024,512]{2,1,0:T(8,128)S(1)} %copy-done.2, f32[2,1024,512]{2,1,0:T(8,128)} %get-tuple-element.33, f32[2,1024,512]{2,1,0:T(8,128)S(1)} %copy-done.4, f32[]{:T(128)S(6)} %div.37, f32[]{:T(128)S(6)} %div.34, ...), kind=kLoop, calls=%fused_computation.26 | loop fusion | flops 23068668 | bytes 50307092 | tf_op jit(solution)/shard_map/reduce_sum | solution.py:112
  274.5 6.7 %all-reduce.18 = (f32[]{:T(128)}, f32[]{:T(128)}, f32[]{:T(128)}, f32[]{:T(128)}) all-reduce(f32[]{:T(128)} %get-tuple-element.3, f32[]{:T(128)} %get-tuple-element.4, f32[]{:T(128)} %get-tuple-element.2, f32[]{:T(128)} %get-tuple-element.39), channel_id=1, replica_groups=mesh['gz_0'=4,'gz_1'=4,'gz_2'=4,'gz_3'=2] {'gz_0'}, use_global_device_ids=true, to_apply=%region_18.0 | all-reduce | flops 4 | bytes 32 | tf_op jit(solution)/shard_map/psum | solution.py:32
  281.2 8.1 %all-reduce.16 = (f32[]{:T(128)}, f32[]{:T(128)}, f32[]{:T(128)}, f32[]{:T(128)}) all-reduce(f32[]{:T(128)} %get-tuple-element.19, f32[]{:T(128)} %get-tuple-element.20, f32[]{:T(128)} %get-tuple-element.21, f32[]{:T(128)} %get-tuple-element.22), channel_id=1, replica_groups=mesh['gz_0'=4,'gz_1'=4,'gz_2'=4,'gz_3'=2] {'gz_1'}, use_global_device_ids=true, to_apply=%region_19.0 | all-reduce | flops 4 | bytes 32 | tf_op jit(solution)/shard_map/psum | solution.py:32
  289.3 12.6 %all-reduce.14 = (f32[]{:T(128)}, f32[]{:T(128)}, f32[]{:T(128)}, f32[]{:T(128)}) all-reduce(f32[]{:T(128)} %get-tuple-element.13, f32[]{:T(128)} %get-tuple-element.14, f32[]{:T(128)} %get-tuple-element.15, f32[]{:T(128)} %get-tuple-element.16), channel_id=1, replica_groups=mesh['gz_0'=4,'gz_1'=4,'gz_2'=4,'gz_3'=2] {'gz_2'}, use_global_device_ids=true, to_apply=%region_20.0 | all-reduce | flops 4 | bytes 32 | tf_op jit(solution)/shard_map/psum | solution.py:32
  302.0 10.1 %all-reduce.20 = (f32[]{:T(128)}, f32[]{:T(128)}, f32[]{:T(128)}, f32[]{:T(128)}) all-reduce(f32[]{:T(128)} %get-tuple-element.7, f32[]{:T(128)} %get-tuple-element.8, f32[]{:T(128)} %get-tuple-element.9, f32[]{:T(128)} %get-tuple-element.10), channel_id=1, replica_groups=mesh['gz_0'=4,'gz_1'=4,'gz_2'=4,'gz_3'=2] {'gz_3'}, use_global_device_ids=true, to_apply=%region_21.0 | all-reduce | flops 4 | bytes 32 | tf_op jit(solution)/shard_map/psum | solution.py:32
  318.0 6.9 %add_multiply_fusion = f32[2,1024,512]{2,1,0:T(8,128)} fusion(f32[2,1024,512]{2,1,0:T(8,128)} %get-tuple-element.33, f32[2,1024,512]{2,1,0:T(8,128)} %get-tuple-element.36, f32[]{:T(128)S(6)} %div.39, f32[]{:T(128)S(6)} %div.41, f32[]{:T(128)S(6)} %div.37, f32[]{:T(128)S(6)} %div.34), kind=kLoop, calls=%fused_computation.28 | loop fusion | flops 6291456 | bytes 12582928 | tf_op jit(solution)/shard_map/mul | solution.py:139
  324.9 1.7 copy-done.10
  326.6 3.0 multiply_divide_fusion
  (34 shorter events, 0.8 us)
Async XLA Ops:
  0.6 3.5 %copy-start.9 = (f32[2,1024,512]{2,1,0:T(8,128)S(1)}, f32[2,1024,512]{2,1,0:T(8,128)}, u32[]{:S(2)}) copy-start(f32[2,1024,512]{2,1,0:T(8,128)} %param.7) | copy-start | bytes 12582916
  4.1 7.9 %copy-start.11 = (s32[2,32,512]{2,1,0:T(8,128)S(1)}, s32[2,32,512]{2,1,0:T(8,128)}, u32[]{:S(2)}) copy-start(s32[2,32,512]{2,1,0:T(8,128)} %param.9) | copy-start | bytes 393220
  5.9 11.7 %copy-start.6 = (f32[2,1024,512]{2,1,0:T(8,128)S(1)}, f32[2,1024,512]{2,1,0:T(8,128)}, u32[]{:S(2)}) copy-start(f32[2,1024,512]{2,1,0:T(8,128)} %param.6) | copy-start | bytes 12582916
  5.9 11.7 %copy-start.8 = (f32[2,1024,512]{2,1,0:T(8,128)S(1)}, f32[2,1024,512]{2,1,0:T(8,128)}, u32[]{:S(2)}) copy-start(f32[2,1024,512]{2,1,0:T(8,128)} %param.5) | copy-start | bytes 12582916
  8.5 88.8 %collective-permute-start.2 = (f32[2,1024,512]{2,1,0:T(8,128)}, f32[2,1024,512]{2,1,0:T(8,128)}, u32[]{:S(2)}, u32[]{:S(2)}) collective-permute-start(f32[2,1024,512]{2,1,0:T(8,128)} %pad_maximum_fusion.4), channel_id=1, source_target_pairs={{1,0},{2,1},{3,2},{4,3},{5,4},{6,5},{7,6},{8,7},{9,8},{10,9},{11,1... | collective-permute-start | bytes 12582920 | tf_op jit(solution)/shard_map/ppermute | solution.py:38
  12.0 74.3 %collective-permute-start = (s32[1,32,512]{2,1,0:T(8,128)S(1)}, s32[1,32,512]{2,1,0:T(8,128)S(1)}, u32[]{:S(2)}, u32[]{:S(2)}) collective-permute-start(s32[1,32,512]{2,1,0:T(8,128)S(1)} %get-tuple-element.62), channel_id=1, source_target_pairs={{0,1},{1,2},{2,3},{3,4},{4,5},{5,6},{6,7},{7,8},{8,9},{9,10},{10,1... | collective-permute-start | bytes 196616 | tf_op jit(solution)/shard_map/ppermute | solution.py:23
  15.6 70.8 %collective-permute-start.1 = (s32[1,32,512]{2,1,0:T(8,128)S(1)}, s32[1,32,512]{2,1,0:T(8,128)S(1)}, u32[]{:S(2)}, u32[]{:S(2)}) collective-permute-start(s32[1,32,512]{2,1,0:T(8,128)S(1)} %get-tuple-element.63), channel_id=1, source_target_pairs={{1,0},{2,1},{3,2},{4,3},{5,4},{6,5},{7,6},{8,7},{9,8},{10,9},{11,1... | collective-permute-start | bytes 196616 | tf_op jit(solution)/shard_map/ppermute | solution.py:26
  77.7 5.4 %copy-start.7 = (f32[2,1024,512]{2,1,0:T(8,128)S(1)}, f32[2,1024,512]{2,1,0:T(8,128)}, u32[]{:S(2)}) copy-start(f32[2,1024,512]{2,1,0:T(8,128)} %param.6) | copy-start | bytes 12582916
  87.3 5.8 %copy-start = (f32[4,1024,512]{2,1,0:T(8,128)}, f32[4,1024,512]{2,1,0:T(8,128)S(1)}, u32[]{:S(2)}) copy-start(f32[4,1024,512]{2,1,0:T(8,128)S(1)} %fusion.1) | copy-start | bytes 25165828
  129.7 8.9 %copy-start.1 = (f32[2,1024,512]{2,1,0:T(8,128)S(1)}, f32[2,1024,512]{2,1,0:T(8,128)}, u32[]{:S(2)}) copy-start(f32[2,1024,512]{2,1,0:T(8,128)} %get-tuple-element.35) | copy-start | bytes 12582916
  132.5 27.6 %collective-permute-start.3 = (f32[1,1024,512]{2,1,0:T(8,128)S(1)}, f32[1,1024,512]{2,1,0:T(8,128)S(1)}, u32[]{:S(2)}, u32[]{:S(2)}) collective-permute-start(f32[1,1024,512]{2,1,0:T(8,128)S(1)} %get-tuple-element.50), channel_id=1, source_target_pairs={{1,0},{2,1},{3,2},{4,3},{5,4},{6,5},{7,6},{8,7},{9,8},{10,9},{11,1... | collective-permute-start | bytes 6291464 | tf_op jit(solution)/shard_map/ppermute | solution.py:26
  134.8 26.5 %collective-permute-start.4 = (f32[1,1024,512]{2,1,0:T(8,128)S(1)}, f32[1,1024,512]{2,1,0:T(8,128)}, u32[]{:S(2)}, u32[]{:S(2)}) collective-permute-start(f32[1,1024,512]{2,1,0:T(8,128)S(1)} %get-tuple-element.51), channel_id=1, source_target_pairs={{0,1},{1,2},{2,3},{3,4},{4,5},{5,6},{6,7},{7,8},{8,9},{9,10},{10,1... | collective-permute-start | bytes 6291464 | tf_op jit(solution)/shard_map/ppermute | solution.py:23
  231.6 27.9 %collective-permute-start.5 = (f32[1,1024,512]{2,1,0:T(8,128)}, f32[1,1024,512]{2,1,0:T(8,128)}, u32[]{:S(2)}, u32[]{:S(2)}) collective-permute-start(f32[1,1024,512]{2,1,0:T(8,128)} %get-tuple-element.44), channel_id=1, source_target_pairs={{1,0},{2,1},{3,2},{4,3},{5,4},{6,5},{7,6},{8,7},{9,8},{10,9},{11,1... | collective-permute-start | bytes 6291464 | tf_op jit(solution)/shard_map/ppermute | solution.py:26
  233.9 26.8 %collective-permute-start.6 = (f32[1,1024,512]{2,1,0:T(8,128)}, f32[1,1024,512]{2,1,0:T(8,128)}, u32[]{:S(2)}, u32[]{:S(2)}) collective-permute-start(f32[1,1024,512]{2,1,0:T(8,128)} %get-tuple-element.45), channel_id=1, source_target_pairs={{0,1},{1,2},{2,3},{3,4},{4,5},{5,6},{6,7},{7,8},{8,9},{9,10},{10,1... | collective-permute-start | bytes 6291464 | tf_op jit(solution)/shard_map/ppermute | solution.py:23
  237.4 23.3 %slice-start = ((s8[8388608]{0:T(1024)(128)(4,1)}), s8[4194304]{0:T(1024)(128)(4,1)S(1)}, s32[]{:S(2)}) async-start(s8[8388608]{0:T(1024)(128)(4,1)} %bitcast.6), calls=%async_computation | async-start | bytes 8388608
  242.3 18.4 %slice-start.1 = ((s8[8388608]{0:T(1024)(128)(4,1)}), s8[4194304]{0:T(1024)(128)(4,1)S(1)}, s32[]{:S(2)}) async-start(s8[8388608]{0:T(1024)(128)(4,1)} %bitcast.6), calls=%async_computation.1 | async-start | bytes 8388608
  242.3 18.4 %copy-start.2 = (f32[2,1024,512]{2,1,0:T(8,128)S(1)}, f32[2,1024,512]{2,1,0:T(8,128)}, u32[]{:S(2)}) copy-start(f32[2,1024,512]{2,1,0:T(8,128)} %get-tuple-element.37) | copy-start | bytes 12582916
  242.3 18.4 %copy-start.4 = (f32[2,1024,512]{2,1,0:T(8,128)S(1)}, f32[2,1024,512]{2,1,0:T(8,128)}, u32[]{:S(2)}) copy-start(f32[2,1024,512]{2,1,0:T(8,128)} %get-tuple-element.34) | copy-start | bytes 12582916
  318.0 6.9 %copy-start.3 = (f32[2,1024,512]{2,1,0:T(8,128)S(1)}, f32[2,1024,512]{2,1,0:T(8,128)}, u32[]{:S(2)}) copy-start(f32[2,1024,512]{2,1,0:T(8,128)} %get-tuple-element.37) | copy-start | bytes 12582916
  318.0 6.9 %copy-start.5 = (f32[2,1024,512]{2,1,0:T(8,128)S(1)}, f32[2,1024,512]{2,1,0:T(8,128)}, u32[]{:S(2)}) copy-start(f32[2,1024,512]{2,1,0:T(8,128)} %get-tuple-element.34) | copy-start | bytes 12582916
  318.0 8.6 %copy-start.10 = (f32[2,1024,512]{2,1,0:T(8,128)S(1)}, f32[2,1024,512]{2,1,0:T(8,128)}, u32[]{:S(2)}) copy-start(f32[2,1024,512]{2,1,0:T(8,128)} %get-tuple-element.31) | copy-start | bytes 12582916
where the time goes:
time: 330 us
  blocking collectives  135 us (41%)
  other arithmetic  82.5 us (25%)
  local copies, waits for them, and re-layouts  53.7 us (16%)
  waiting for transfers between devices  27.3 us (8%)
  starting transfers between devices  20.8 us (6%)
  between operations  10.6 us (3%)
    psum x8, blocking collectives, by_axis(): return functools.reduce(lax.psum, axes, x)  79.2 us
    pmax x4, blocking collectives, over_axes(): x = lax.pmax(x, axis)  55.5 us
    mul x2, other arithmetic, apply_operator(): masked = search * fluid_cells  36.5 us
    slice x8, local copies, waits for them, and re-layouts, later_cells(): tail = lax.slice_in_dim(field, 1, size, axis=axis)  36 us
    ppermute x3, waiting for transfers between devices, with_halo(): lax.ppermute(lax.slice_in_dim(block, 0, width, axis=dim), axis, backward)  24.9 us
    reduce_sum x1, other arithmetic, paired_sums(): jnp.sum(image * precond)  16.2 us
    reduce_sum x1, other arithmetic, local(): div_part = jnp.sum(divergence * divergence)  13.8 us
    ppermute x3, starting transfers between devices, with_halo(): lax.ppermute(lax.slice_in_dim(block, block.shape[dim] - width, None, axis...  10.8 us
  transfers between devices with their start and end apart: 7, of which 4 were waited for; matrix products, arithmetic and copies ran while one was open for 12% of the time, Pallas kernels for 0%

commit v1 on v0

v1 whole, which is shorter than its diff:
```python
import functools

import jax
import jax.numpy as jnp
from jax import lax
from jax.experimental import pallas as pl
from jax.experimental.pallas import tpu as pltpu
from jax.sharding import PartitionSpec as P

EPS = 1e-06
CFL = 0.5
BUOYANCY = 100.0
MESH = pl.DeviceIdType.MESH

R = 32
CH = 64
LOAD = 256
PAD = 8
STAGES = ((1, 8, 0), (8, 4, 8), (32, 4, 12))
SLOTS = 16


def kernel(
    planes, rows, cols, devices,
    u_hbm, v_hbm, w_hbm, s_hbm, o_hbm, imp, rel,
    U, V, W, SM, FL, CNT, Z0, Z1, G, H, RED, ACC,
    load_sem, flag_sem, fs, fr, bs, br, lws, lwr, z0ds, z0dr, z1ds, z1dr, z0us, z0ur, z1us, z1ur,
    reds, redr,
):
    me = lax.axis_index("gz")
    low, high = me - 1, me + 1
    has_low, has_high = me > 0, me < devices - 1
    chunks = rows // CH
    early = chunks // 4
    loads = rows // LOAD
    lane = lax.broadcasted_iota(jnp.int32, (R, cols), 1)

    def peer(stride, n, k):
        pos = lax.rem(lax.div(me, stride), n)
        return me + (lax.rem(pos + k, n) - pos) * stride

    def load(a, p, q):
        src = (u_hbm, v_hbm, w_hbm, s_hbm)[a]
        dst = (U, V, W, SM)[a]
        span = pl.ds(q * LOAD, LOAD)
        return pltpu.make_async_copy(src.at[p, span], dst.at[p, span], load_sem.at[a, p, q])

    for p in range(planes):
        for q in range(loads):
            for a in range(3):
                load(a, p, q).start()
    flags_in = pltpu.make_async_copy(o_hbm, FL.at[pl.ds(1, planes)], flag_sem)
    flags_in.start()
    for p in range(planes):
        for q in range(loads):
            load(3, p, q).start()

    barrier = pltpu.get_barrier_semaphore()
    peers = 0
    for stride, n, _ in STAGES:
        for k in range(1, n):
            peers += 1
            pl.semaphore_signal(barrier, inc=1, device_id=(peer(stride, n, k),), device_id_type=MESH)

    @pl.when(has_low)
    def _():
        pl.semaphore_signal(barrier, inc=1, device_id=(low,), device_id_type=MESH)

    @pl.when(has_high)
    def _():
        pl.semaphore_signal(barrier, inc=1, device_id=(high,), device_id_type=MESH)

    V[:, pl.ds(rows, PAD), :] = jnp.zeros((planes, PAD, cols), jnp.float32)
    for Z in (Z0, Z1):
        for p in (1, 2):
            Z[p, pl.ds(0, PAD), :] = jnp.zeros((PAD, cols), jnp.float32)
            Z[p, pl.ds(PAD + rows, PAD), :] = jnp.zeros((PAD, cols), jnp.float32)

    def blocks(body, carry, first=0, last=rows // R):
        return lax.fori_loop(first, last, lambda b, c: body(pl.multiple_of(b * R, R), c), carry)

    def clear(refs):
        def body(r, c):
            for ref in refs:
                ref[pl.ds(r, R), :] = jnp.zeros((R, cols), jnp.float32)
            return c

        blocks(body, 0)

    @pl.when(jnp.logical_not(has_low))
    def _():
        FL[0] = jnp.zeros(FL.shape[1:], jnp.int32)
        for Z in (Z0, Z1):
            clear([Z.at[0, pl.ds(PAD, rows)]])

    @pl.when(jnp.logical_not(has_high))
    def _():
        FL[3] = jnp.zeros(FL.shape[1:], jnp.int32)
        clear([W.at[2], SM.at[2], Z0.at[3, pl.ds(PAD, rows)], Z1.at[3, pl.ds(PAD, rows)]])

    sides = jnp.where(has_low, 1, 0) + jnp.where(has_high, 1, 0)
    pl.semaphore_wait(barrier, peers + sides)

    def remote(src, dst, ss, rs, dev):
        return pltpu.make_async_remote_copy(
            src_ref=src, dst_ref=dst, send_sem=ss, recv_sem=rs, device_id=(dev,), device_id_type=MESH
        )

    def span(c, pad):
        return pl.ds(pl.multiple_of(c * CH + pad, 8), CH)

    def flags_copy(up):
        if up:
            return remote(o_hbm.at[planes - 1], FL.at[0], fs.at[0], fr.at[0], high)
        return remote(o_hbm.at[0], FL.at[3], fs.at[1], fr.at[1], low)

    def early_copy(a, c):
        src, dst = ((w_hbm, W), (s_hbm, SM))[a]
        return remote(src.at[0, span(c, 0)], dst.at[2, span(c, 0)], bs.at[a, c], br.at[a, c], low)

    def lw_copy(c):
        return remote(W.at[0, span(c, 0)], W.at[2, span(c, 0)], lws.at[c], lwr.at[c], low)

    def z_copy(Z, up, c):
        if up:
            ss, rs = (z0us, z0ur) if Z is Z0 else (z1us, z1ur)
            return remote(Z.at[2, span(c, PAD)], Z.at[0, span(c, PAD)], ss.at[c], rs.at[c], high)
        ss, rs = (z0ds, z0dr) if Z is Z0 else (z1ds, z1dr)
        return remote(Z.at[1, span(c, PAD)], Z.at[3, span(c, PAD)], ss.at[c], rs.at[c], low)

    def each(first, last, body):
        lax.fori_loop(first, last, lambda c, x: (body(c), x)[1], 0)

    @pl.when(has_low)
    def _():
        flags_copy(False).start()

        def body(c):
            early_copy(0, c).start()
            early_copy(1, c).start()

        each(0, early, body)

    @pl.when(has_high)
    def _():
        flags_copy(True).start()

    def red_copy(i, s, k, n_rows):
        stride, n, base = STAGES[s]
        part = pl.ds(0, n_rows)
        return remote(
            RED.at[i, base, part], RED.at[i, base + k, part], reds.at[i, base + k], redr.at[i, base + k],
            peer(stride, n, k),
        )

    def red_send(i, s, value):
        n_rows = value.shape[0]
        RED[i, STAGES[s][2], pl.ds(0, n_rows), :] = value
        for k in range(1, STAGES[s][1]):
            red_copy(i, s, k, n_rows).start()

    def red_wait(i, s, n_rows, op):
        _, n, base = STAGES[s]
        for k in range(1, n):
            red_copy(i, s, k, n_rows).wait_recv()
        total = RED[i, base, pl.ds(0, n_rows), :]
        for k in range(1, n):
            total = op(total, RED[i, base + k, pl.ds(0, n_rows), :])
        return total

    def red_end(i, n_rows):
        for s in range(3):
            for k in range(1, STAGES[s][1]):
                red_copy(i, s, k, n_rows).wait_send()

    def fold(x, op=jnp.add):
        return functools.reduce(op, [x[8 * i : 8 * i + 8] for i in range(x.shape[0] // 8)])

    def lanes(x, op=jnp.add):
        return functools.reduce(op, [x[:, 128 * i : 128 * i + 128] for i in range(x.shape[1] // 128)])

    def full(x):
        return jnp.full((8, 128), x, jnp.float32)

    top = jnp.zeros((8, cols), jnp.float32)
    for p in range(planes):
        for q in range(loads):
            for a in range(3):
                load(a, p, q).wait()

            def body(r, acc, p=p):
                m = jnp.maximum(
                    jnp.maximum(jnp.abs(U[p, pl.ds(r, R), :]), jnp.abs(V[p, pl.ds(r, R), :])),
                    jnp.abs(W[p, pl.ds(r, R), :]),
                )
                return jnp.maximum(acc, fold(m, jnp.maximum))

            top = blocks(body, top, q * LOAD // R, (q + 1) * LOAD // R)
    red_send(0, 0, lanes(top, jnp.maximum))

    flags_in.wait()

    @pl.when(has_low)
    def _():
        flags_copy(True).wait_recv()

    @pl.when(has_high)
    def _():
        flags_copy(False).wait_recv()

    words = rows // 32
    w_lane = lax.broadcasted_iota(jnp.int32, (words, cols), 1)
    w_row = lax.broadcasted_iota(jnp.int32, (words, cols), 0)
    for p in range(planes):
        c = FL[p + 1]
        zero = jnp.zeros_like(c)
        left = jnp.where(w_lane == 0, zero, pltpu.roll(c, 1, 1))
        right = jnp.where(w_lane == cols - 1, zero, pltpu.roll(c, cols - 1, 1))
        before = jnp.where(w_row == 0, zero, pltpu.roll(c, 1, 0))
        after = jnp.where(w_row == words - 1, zero, pltpu.roll(c, words - 1, 0))
        back = jnp.left_shift(c, 1) | lax.shift_right_logical(before, jnp.full_like(c, 31))
        ahead = lax.shift_right_logical(c, jnp.full_like(c, 1)) | jnp.left_shift(after, 31)
        below, above = FL[p], FL[p + 2]
        s1 = left ^ right ^ back
        c1 = (left & right) | (back & (left ^ right))
        s2 = ahead ^ below ^ above
        c2 = (ahead & below) | (above & (ahead ^ below))
        c3 = s1 & s2
        CNT[0, p] = s1 ^ s2
        CNT[1, p] = c1 ^ c2 ^ c3
        CNT[2, p] = (c1 & c2) | (c3 & (c1 ^ c2))
    for q in range(loads):
        for p in range(planes):
            load(3, p, q).wait()

    part = red_wait(0, 0, 8, jnp.maximum)
    red_send(0, 1, part)
    part = red_wait(0, 1, 8, jnp.maximum)
    red_send(0, 2, part)
    part = red_wait(0, 2, 8, jnp.maximum)
    step_v = CFL / (full(jnp.max(part)) + EPS)
    time_step = step_v[0, 0]
    lift = (step_v * BUOYANCY)[0, 0]
    per_step = (1.0 / step_v)[0, 0]

    def lift_block(p):
        def body(r, c):
            rs = pl.ds(r, R)
            W[p, rs, :] = W[p, rs, :] + lift * SM[p, rs, :]
            return c

        return body

    per = CH // R

    def lift_send(c):
        blocks(lift_block(0), 0, c * per, (c + 1) * per)

        @pl.when(has_low)
        def _():
            lw_copy(c).start()

    each(early, chunks, lift_send)
    blocks(lift_block(0), 0, 0, early * per)
    blocks(lift_block(1), 0)

    bit = lax.broadcasted_iota(jnp.int32, (R, cols), 0)

    def flag_block(p):
        def body(b, c):
            def bits(ref):
                return jnp.right_shift(jnp.broadcast_to(ref, (R, cols)), bit) & 1

            one = pl.ds(b, 1)
            solid = bits(FL[p + 1, one, :])
            count = (
                bits(CNT[0, p, one, :])
                + jnp.left_shift(bits(CNT[1, p, one, :]), 1)
                + jnp.left_shift(bits(CNT[2, p, one, :]), 2)
            )
            opened = (6 - count).astype(jnp.float32)
            wet = solid == 0
            rs = pl.ds(pl.multiple_of(b * R, R), R)
            H[p, rs, :] = jnp.where(wet, opened, 0.0)
            G[p, rs, :] = jnp.where(wet, 1.0 / jnp.maximum(opened, 1.0), 0.0)
            return c

        lax.fori_loop(0, rows // R, body, 0)

    def to_right(x):
        return jnp.where(lane == 0, 0.0, pltpu.roll(x, 1, 1))

    def to_left(x):
        return jnp.where(lane == cols - 1, 0.0, pltpu.roll(x, cols - 1, 1))

    def rhs_block(p):
        def body(r, acc):
            div_sum, wet_sum, gamma = acc
            rs = pl.ds(r, R)
            u, g = U[p, rs, :], G[p, rs, :]
            vb = V[p, pl.ds(r, R + PAD), :]
            v_next = pltpu.roll(vb, R + PAD - 1, 0)[:R]
            flat = (to_left(u) - u) + (v_next - vb[:R])
            wet = g > 0.0
            div = jnp.where(wet, flat + (W[p + 1, rs, :] - W[p, rs, :]), 0.0)
            r0 = div * per_step
            z0 = g * r0
            Z0[p + 1, pl.ds(pl.multiple_of(r + PAD, 8), R), :] = z0
            return (
                div_sum + fold(div * div),
                wet_sum + fold(jnp.where(wet, 1.0, 0.0)),
                gamma + fold(r0 * z0),
            )

        return body

    def chunk_loop(body, carry):
        return lax.fori_loop(0, chunks, body, carry)

    nil = jnp.zeros((8, cols), jnp.float32)
    flag_block(0)

    def first_rhs(c, acc):
        acc = blocks(rhs_block(0), acc, c * per, (c + 1) * per)

        @pl.when(has_low)
        def _():
            z_copy(Z0, False, c).start()

        return acc

    acc = chunk_loop(first_rhs, (nil, nil, nil))
    flag_block(1)

    @pl.when(has_high)
    def _():
        def body(c):
            early_copy(0, c).wait_recv()
            early_copy(1, c).wait_recv()

        each(0, early, body)

    blocks(lift_block(2), 0, 0, early * per)

    def second_rhs(c, acc):
        @pl.when(jnp.logical_and(has_high, c >= early))
        def _():
            lw_copy(c).wait_recv()

        acc = blocks(rhs_block(1), acc, c * per, (c + 1) * per)

        @pl.when(has_high)
        def _():
            z_copy(Z0, True, c).start()

        return acc

    div_sum, wet_sum, gamma = chunk_loop(second_rhs, acc)

    def around(Z, p, r):
        zb = Z[p, pl.ds(r, R + 2 * PAD), :]
        z = zb[PAD : PAD + R]
        n = R + 2 * PAD
        beside = pltpu.roll(zb, 1, 0)[PAD : PAD + R] + pltpu.roll(zb, n - 1, 0)[PAD : PAD + R]
        return z, beside + (to_right(z) + to_left(z))

    def image_block(r, delta):
        rs, rp = pl.ds(r, R), pl.ds(pl.multiple_of(r + PAD, 8), R)
        a, a_in = around(Z0, 1, r)
        b, b_in = around(Z0, 2, r)
        under = Z0[0, rp, :]
        image_a = H[0, rs, :] * a - (a_in + b + under)
        image_b = H[1, rs, :] * b - (b_in + a)
        Z1[1, rp, :] = G[0, rs, :] * image_a
        Z1[2, rp, :] = image_b
        return delta + fold(a * (image_a - under) + b * image_b)

    def first_image(c, delta):
        @pl.when(has_low)
        def _():
            z_copy(Z0, True, c).wait_recv()

        delta = blocks(image_block, delta, c * per, (c + 1) * per)

        @pl.when(has_low)
        def _():
            z_copy(Z1, False, c).start()

        return delta

    delta = chunk_loop(first_image, nil)
    red_send(1, 0, jnp.concatenate([lanes(x) for x in (div_sum, wet_sum, gamma, delta)], 0))

    def second_image(first, last):
        def body(c, x):
            @pl.when(has_high)
            def _():
                z_copy(Z0, False, c).wait_recv()

            def block(r, x):
                rs, rp = pl.ds(r, R), pl.ds(pl.multiple_of(r + PAD, 8), R)
                Z1[2, rp, :] = G[1, rs, :] * (Z1[2, rp, :] - Z0[3, rp, :])
                return x

            blocks(block, 0, c * per, (c + 1) * per)

            @pl.when(has_high)
            def _():
                z_copy(Z1, True, c).start()

            return x

        lax.fori_loop(first, last, body, 0)

    quarter = chunks // 4
    second_image(0, quarter)
    part = red_wait(1, 0, 32, jnp.add)
    red_send(1, 1, part)
    second_image(quarter, 2 * quarter)
    part = red_wait(1, 1, 32, jnp.add)
    red_send(1, 2, part)
    second_image(2 * quarter, 3 * quarter)
    part = red_wait(1, 2, 32, jnp.add)
    second_image(3 * quarter, chunks)
    div_squares = full(jnp.sum(part[0:8]))
    fluid_total = jnp.maximum(full(jnp.sum(part[8:16])), 1.0)
    gamma_0 = full(jnp.sum(part[16:24]))
    delta_0 = full(jnp.sum(part[24:32]))
    alpha_v = gamma_0 / delta_0
    alpha = alpha_v[0, 0]

    A2 = U

    def inner_block(r, acc):
        gamma, delta = acc
        rs, rp = pl.ds(r, R), pl.ds(pl.multiple_of(r + PAD, 8), R)
        a, a_in = around(Z1, 1, r)
        b, b_in = around(Z1, 2, r)
        under = Z1[0, rp, :]
        h_a, h_b = H[0, rs, :], H[1, rs, :]
        image_a = jnp.where(G[0, rs, :] > 0.0, h_a * a - (a_in + b + under), 0.0)
        image_b = jnp.where(G[1, rs, :] > 0.0, h_b * b - (b_in + a), 0.0)
        A2[0, rs, :] = image_a
        A2[1, rs, :] = image_b
        s_a, s_b = jnp.maximum(h_a, 1.0), jnp.maximum(h_b, 1.0)
        y_a = Z0[1, rp, :] - alpha * a
        y_b = Z0[2, rp, :] - alpha * b
        y_under = Z0[0, rp, :] - alpha * under
        gamma = gamma + fold(s_a * (y_a * y_a) + s_b * (y_b * y_b))
        t_a = (s_a * a - alpha * image_a) - y_under
        t_b = (s_b * b - alpha * image_b) + Z0[3, rp, :]
        delta = delta + fold(y_a * t_a + y_b * t_b)
        return gamma, delta

    def inner(c, acc):
        @pl.when(has_low)
        def _():
            z_copy(Z1, True, c).wait_recv()

        return blocks(inner_block, acc, c * per, (c + 1) * per)

    gamma, delta = chunk_loop(inner, (nil, nil))
    red_send(2, 0, jnp.concatenate([lanes(gamma), lanes(delta)], 0))
    part = red_wait(2, 0, 16, jnp.add)
    red_send(2, 1, part)
    part = red_wait(2, 1, 16, jnp.add)
    red_send(2, 2, part)
    part = red_wait(2, 2, 16, jnp.add)
    gamma_1 = full(jnp.sum(part[0:8]))
    delta_1 = full(jnp.sum(part[8:16]))
    beta = gamma_1 / gamma_0
    alpha_1 = gamma_1 / (delta_1 - beta * gamma_1 / alpha_v)
    c0_v = alpha_v + alpha_1 * (1.0 + beta)
    c1_v = -(alpha_v * alpha_1)
    scale_v = step_v / jnp.sqrt(div_squares / fluid_total + EPS)
    c0, c1, scale = c0_v[0, 0], c1_v[0, 0], scale_v[0, 0]

    def out_block(p, with_above):
        def body(r, x):
            rs, rp = pl.ds(r, R), pl.ds(pl.multiple_of(r + PAD, 8), R)
            z0, z1 = Z0[p + 1, rp, :], Z1[p + 1, rp, :]
            imp[p, rs, :] = time_step * (c0 * z0 + c1 * z1)
            second = A2[p, rs, :]
            if with_above:
                second = second - jnp.where(G[p, rs, :] > 0.0, Z1[3, rp, :], 0.0)
            rel[p, rs, :] = scale * (jnp.maximum(H[p, rs, :], 1.0) * (z0 - c0 * z1) - c1 * second)
            return x

        return body

    blocks(out_block(0, False), 0)

    def last(c, x):
        @pl.when(has_high)
        def _():
            z_copy(Z1, False, c).wait_recv()

        blocks(out_block(1, True), 0, c * per, (c + 1) * per)
        return x

    chunk_loop(last, 0)

    @pl.when(has_low)
    def _():
        flags_copy(False).wait_send()

        def sent_early(c):
            early_copy(0, c).wait_send()
            early_copy(1, c).wait_send()

        each(0, early, sent_early)
        each(early, chunks, lambda c: lw_copy(c).wait_send())

        def sent(c):
            z_copy(Z0, False, c).wait_send()
            z_copy(Z1, False, c).wait_send()

        each(0, chunks, sent)

    @pl.when(has_high)
    def _():
        flags_copy(True).wait_send()

        def sent(c):
            z_copy(Z0, True, c).wait_send()
            z_copy(Z1, True, c).wait_send()

        each(0, chunks, sent)

    red_end(0, 8)
    red_end(1, 32)
    red_end(2, 16)


def local(devices, u_face, v_face, w_face, smoke, obstacles):
    planes, rows, cols = u_face.shape
    chunks, early, loads = rows // CH, rows // CH // 4, rows // LOAD
    f32 = jnp.float32
    dma = pltpu.SemaphoreType.DMA
    out = jax.ShapeDtypeStruct((planes, rows, cols), f32)
    hbm = pl.BlockSpec(memory_space=pl.ANY)
    return pl.pallas_call(
        functools.partial(kernel, planes, rows, cols, devices),
        out_shape=(out, out),
        in_specs=[hbm] * 5,
        out_specs=(pl.BlockSpec(memory_space=pltpu.VMEM),) * 2,
        scratch_shapes=[
            pltpu.VMEM((planes, rows, cols), f32),
            pltpu.VMEM((planes, rows + PAD, cols), f32),
            pltpu.VMEM((planes + 1, rows, cols), f32),
            pltpu.VMEM((planes + 1, rows, cols), f32),
            pltpu.VMEM((planes + 2, rows // 32, cols), jnp.int32),
            pltpu.VMEM((3, planes, rows // 32, cols), jnp.int32),
            pltpu.VMEM((planes + 2, rows + 2 * PAD, cols), f32),
            pltpu.VMEM((planes + 2, rows + 2 * PAD, cols), f32),
            pltpu.VMEM((planes, rows, cols), f32),
            pltpu.VMEM((planes, rows, cols), f32),
            pltpu.VMEM((3, SLOTS, 32, 128), f32),
            pltpu.VMEM((8, 128), f32),
            dma((4, planes, loads)),
            dma,
            dma((2,)), dma((2,)),
            dma((2, early)), dma((2, early)),
            dma((chunks,)), dma((chunks,)),
            dma((chunks,)), dma((chunks,)),
            dma((chunks,)), dma((chunks,)),
            dma((chunks,)), dma((chunks,)),
            dma((chunks,)), dma((chunks,)),
            dma((3, SLOTS)), dma((3, SLOTS)),
        ],
        compiler_params=pltpu.CompilerParams(
            collective_id=0, has_side_effects=True, vmem_limit_bytes=67043328
        ),
        name="step",
    )(u_face, v_face, w_face, smoke, obstacles)


def solution(mesh):
    spec = P("gz", None, None)
    return jax.shard_map(
        functools.partial(local, mesh.shape["gz"]),
        mesh=mesh,
        in_specs=(spec,) * 5,
        out_specs=(spec, spec),
        check_vma=False,
    )
```

time: 330 us -> 151 us (0.46)
  Pallas kernels: 0 us -> 142 us
  blocking collectives: 135 us -> 0 us
  other arithmetic: 82.5 us -> 0 us
  local copies, waits for them, and re-layouts: 53.7 us -> 6.84 us
  waiting for transfers between devices: 27.3 us -> 0 us
  starting transfers between devices: 20.8 us -> 0 us
  between operations: 10.6 us -> 0.65 us
    pallas_call x0 -> x1, Pallas kernels: none -> 142 us  [local(): pl.pallas_call(functools.partial(kernel, planes, rows, cols, devices), ou...]
    psum x8 -> x0, blocking collectives: 79.2 us -> none  [by_axis(): return functools.reduce(lax.psum, axes, x)]
    pmax x4 -> x0, blocking collectives: 55.5 us -> none  [over_axes(): x = lax.pmax(x, axis)]
    slice x14 -> x0, local copies, waits for them, and re-layouts: 50.6 us -> none  [the longest x8 36 us: later_cells(): tail = lax.slice_in_dim(field, 1, size, axis=axis)]
    mul x3 -> x0, other arithmetic: 43.3 us -> none  [the longest x2 36.5 us: apply_operator(): masked = search * fluid_cells]
    reduce_sum x2 -> x0, other arithmetic: 30 us -> none  [the longest x1 16.2 us: paired_sums(): jnp.sum(image * precond)]
    ppermute x7 -> x0, waiting for transfers between devices: 27.3 us -> none  [the longest x3 24.9 us: with_halo(): lax.ppermute(lax.slice_in_dim(block, 0, width, axis=dim), axis, backward)]
    ppermute x7 -> x0, starting transfers between devices: 20.8 us -> none  [the longest x3 10.8 us: with_halo(): lax.ppermute(lax.slice_in_dim(block, block.shape[dim] - width, None, axis...]
  transfers between devices with their start and end apart: 7 -> 0, of which waited for: 4 -> 0; matrix products, arithmetic and copies ran while one was open for 12% -> 0% of each run, Pallas kernels for 0% -> 0%
where the time goes in v1:
time: 151 us; the launch traced here: 150 us
  Pallas kernels  142 us (94%)
  local copies, waits for them, and re-layouts  6.84 us (5%)
    pallas_call x1, Pallas kernels, local(): pl.pallas_call(functools.partial(kernel, planes, rows, cols, devices), ou...  142 us
    unnamed x4, local copies, waits for them, and re-layouts  6.84 us

profile of v1, /device:TPU:1, one launch (start us, length us, event | category | flops | bytes accessed | tf_op | source)
XLA Modules:
  0.0 149.8 jit_solution(10205717327748966030)
XLA Ops:
  0.6 142.4 %step.1 = (f32[2,1024,512]{2,1,0:T(8,128)}, f32[2,1024,512]{2,1,0:T(8,128)}) custom-call(f32[2,1024,512]{2,1,0:T(8,128)} %u_hbm.1, f32[2,1024,512]{2,1,0:T(8,128)} %v_hbm.1, f32[2,1024,512]{2,1,0:T(8,128)} %w_hbm.1, f32[2,1024,512]{2,1,0:T(8,128)} %s_hbm.1, s32[2,32,512]{2,1,0:T(8,128)} %o_hbm.1), custom_call_target="tpu_custom_call" | custom-call | tf_op jit(solution)/shard_map/step/pallas_call | solution.py:542
  143.0 0.0 copy-start
  143.0 4.8 %copy.9 = f32[2,1024,512]{2,1,0:T(8,128)} copy(f32[2,1024,512]{2,1,0:T(8,128)} %get-tuple-element.4) | data formatting | bytes 8388608
  147.8 0.0 copy-done
  147.8 2.0 %copy.10 = f32[2,1024,512]{2,1,0:T(8,128)} copy(f32[2,1024,512]{2,1,0:T(8,128)S(1)} %copy-done) | data formatting | bytes 8388608
Async XLA Ops:
  143.0 4.8 %copy-start = (f32[2,1024,512]{2,1,0:T(8,128)S(1)}, f32[2,1024,512]{2,1,0:T(8,128)}, u32[]{:S(2)}) copy-start(f32[2,1024,512]{2,1,0:T(8,128)} %get-tuple-element.5) | copy-start | bytes 12582916
